TPU v7x, 32 devices: a whole 2x2x4 slice. The times are simulated.
32 devices in a mesh: dp: 8 (over z, x), expert: 4 (over y, core).
Axes of the slice: x: 2, y: 2, z: 4, core: 2. Of those that a mesh axis runs over, the one named last changes fastest.
Arguments:
- tokens: bfloat16 [4096, 2048], P(('dp', 'expert')), may hold values from -6 to 6
- out_grad: bfloat16 [4096, 2048], P(('dp', 'expert')), may hold values from -3 to 3
- z_weight: float32 [4096], P(('dp', 'expert')), may hold values from 0.1 to 1
- router_weight: bfloat16 [2048, 128], replicated, may hold values from -0.125 to 0.125
- expert_ids: int32 [4096, 4], P(('dp', 'expert')), may hold values from 0 to 127, as said below
- gate_up_weight: bfloat16 [4, 2048, 3072], P('expert'), may hold values from -0.125 to 0.125
- down_weight: bfloat16 [4, 1536, 2048], P('expert'), may hold values from -0.15625 to 0.15625
Outputs:
- token_grad: bfloat16 [4096, 2048], P(('dp', 'expert'))
- router_grad: float32 [2048, 128], replicated
- gate_up_grad: bfloat16 [4, 2048, 3072], P('expert', 'dp')
- down_grad: bfloat16 [4, 1536, 2048], P('expert', 'dp')
Inputs may be any that keep to these rules, and one draw needn't show every extreme that they name: `expert_ids`: each row names 4 different experts. Experts 0 to 3 are the ones in flight. The 128 rows of one device name any one expert in flight at most 64 times; in every data group some expert in flight is named exactly 64 times by the rows of each device of the group.
All inputs are finite; a program needn't handle non-finite values.
Results may differ from a plain program's by a relative error of at most 0.019.
Values may be sent and summed in bfloat16 or wider, within the bound.
A program may use at most 192 MiB of HBM per device.

v0:
```python
import jax
import jax.numpy as jnp
from jax import lax
from jax.sharding import PartitionSpec as P


def expert_rows(rows_in, rows_grad, w_gateup, w_down, acc_gateup, acc_down):
    hidden_units = w_down.shape[0]
    pre_act = jnp.dot(rows_in, w_gateup, preferred_element_type=jnp.float32)
    gate_pre = pre_act[:, :hidden_units]
    up_pre = pre_act[:, hidden_units:]
    activated = jax.nn.silu(gate_pre)
    hidden = (activated * up_pre).astype(jnp.bfloat16)
    expert_out = jnp.dot(hidden, w_down, preferred_element_type=jnp.float32).astype(jnp.bfloat16)
    hidden_grad = lax.dot_general(
        rows_grad, w_down, (((1,), (1,)), ((), ())), preferred_element_type=jnp.float32
    )
    acc_down = lax.dot_general(
        hidden, rows_grad, (((0,), (0,)), ((), ())), preferred_element_type=jnp.float32
    )
    sigmoid_gate = jax.nn.sigmoid(gate_pre)
    gate_grad = hidden_grad * up_pre * sigmoid_gate * (1.0 + gate_pre * (1.0 - sigmoid_gate))
    up_grad = hidden_grad * activated
    pre_grad = jnp.concatenate([gate_grad, up_grad], axis=1).astype(jnp.bfloat16)
    acc_gateup = lax.dot_general(
        rows_in, pre_grad, (((0,), (0,)), ((), ())), preferred_element_type=jnp.float32
    )
    input_grad = lax.dot_general(
        pre_grad, w_gateup, (((1,), (1,)), ((), ())), preferred_element_type=jnp.float32
    ).astype(jnp.bfloat16)
    return (acc_gateup, acc_down, expert_out, input_grad)


def split_pair(values):
    upper = values.astype(jnp.bfloat16)
    lower = (values - upper.astype(jnp.float32)).astype(jnp.bfloat16)
    return jnp.stack([upper, lower], axis=-1)


def join_pair(pair):
    return pair[..., 0].astype(jnp.float32) + pair[..., 1].astype(jnp.float32)


def per_device(tokens, out_grad, z_weight, router_weight, expert_ids, gate_up_weight, down_weight):
    tok_count, width = tokens.shape
    top_count = expert_ids.shape[1]
    routed = router_weight.shape[1]
    flight = lax.axis_size("expert")
    capacity = tok_count // 2
    w_gateup = gate_up_weight[0]
    w_down = down_weight[0]
    hidden_units = w_down.shape[0]
    logits = jnp.dot(tokens, router_weight, preferred_element_type=jnp.float32)
    choose = expert_ids[:, :, None] == jnp.arange(routed, dtype=jnp.int32)[None, None, :]
    selected = jnp.sum(jnp.where(choose, logits[:, None, :], 0.0), axis=2)
    sel_exp = jnp.exp(selected)
    probs = sel_exp / jnp.sum(sel_exp, axis=1, keepdims=True)
    log_total = jnp.log(jnp.sum(jnp.exp(logits), axis=1))
    flat_ids = expert_ids.reshape(-1)
    slot_count = tok_count * top_count
    member = (flat_ids[:, None] == jnp.arange(flight, dtype=jnp.int32)[None, :]).astype(jnp.int32)
    ranks = jnp.sum((jnp.cumsum(member, axis=0) - 1) * member, axis=1)
    in_flight = flat_ids < flight
    position = jnp.where(in_flight, flat_ids * capacity + ranks, flight * capacity)
    source_slot = (
        jnp.zeros((flight * capacity,), jnp.int32)
        .at[position]
        .set(jnp.arange(slot_count, dtype=jnp.int32), mode="drop")
    )
    filled = jnp.zeros((flight * capacity,), jnp.bool_).at[position].set(True, mode="drop")
    source_tok = source_slot // top_count
    send_in = jnp.where(filled[:, None], tokens[source_tok], 0)
    slot_prob = jnp.where(filled, probs.reshape(-1)[source_slot], 0.0)
    counts = jnp.sum(member, axis=0)
    count_msg = jnp.stack([counts // 128, counts % 128], axis=1).astype(jnp.bfloat16)
    send_raw = jnp.where(filled[:, None], out_grad[source_tok], 0)
    prob_pair = split_pair(slot_prob)
    recv_in, recv_raw, recv_prob, recv_counts = (
        lax.all_to_all(
            send_in.reshape(flight, capacity, width),
            "expert",
            split_axis=0,
            concat_axis=0,
            tiled=True,
        ),
        lax.all_to_all(
            send_raw.reshape(flight, capacity, width),
            "expert",
            split_axis=0,
            concat_axis=0,
            tiled=True,
        ),
        lax.all_to_all(
            prob_pair.reshape(flight, capacity, 2),
            "expert",
            split_axis=0,
            concat_axis=0,
            tiled=True,
        ),
        lax.all_to_all(count_msg, "expert", split_axis=0, concat_axis=0, tiled=True),
    )
    sources = recv_in.shape[0]
    total_rows = sources * capacity
    flat_in = recv_in.reshape(total_rows, width)
    flat_raw = recv_raw.reshape(total_rows, width)
    row_prob = join_pair(recv_prob.reshape(total_rows, 2))
    flat_grad = (row_prob[:, None] * flat_raw.astype(jnp.float32)).astype(jnp.bfloat16)
    acc_gateup, acc_down, produced, back_rows = expert_rows(
        flat_in,
        flat_grad,
        w_gateup,
        w_down,
        jnp.zeros((width, 2 * hidden_units), jnp.float32),
        jnp.zeros((hidden_units, width), jnp.float32),
    )
    slot_at = jnp.where(in_flight, position, 0)
    row_score = jnp.sum(flat_raw.astype(jnp.float32) * produced.astype(jnp.float32), axis=1)
    score_pair = split_pair(row_score)
    home_dx, home_pair = (
        lax.all_to_all(
            back_rows.reshape(sources, capacity, width),
            "expert",
            split_axis=0,
            concat_axis=0,
            tiled=True,
        ),
        lax.all_to_all(
            score_pair.reshape(sources, capacity, 2),
            "expert",
            split_axis=0,
            concat_axis=0,
            tiled=True,
        ),
    )
    flat_dx = home_dx.reshape(flight * capacity, width)
    flat_score = join_pair(home_pair.reshape(flight * capacity, 2))
    scores = jnp.where(in_flight, flat_score[slot_at], 0.0).reshape(tok_count, top_count)
    slot_dx = jnp.where(in_flight[:, None], flat_dx[slot_at], 0).reshape(
        tok_count, top_count, width
    )
    mean_score = jnp.sum(probs * scores, axis=1, keepdims=True)
    sel_grad = probs * (scores - mean_score)
    z_grad = 2.0 * z_weight[:, None] * log_total[:, None] * jnp.exp(logits - log_total[:, None])
    logit_grad = (z_grad + jnp.sum(jnp.where(choose, sel_grad[:, :, None], 0.0), axis=1)).astype(
        jnp.bfloat16
    )
    token_grad = (
        jnp.sum(slot_dx.astype(jnp.float32), axis=1)
        + lax.dot_general(
            logit_grad, router_weight, (((1,), (1,)), ((), ())), preferred_element_type=jnp.float32
        )
    ).astype(jnp.bfloat16)
    router_part = lax.dot_general(
        tokens, logit_grad, (((0,), (0,)), ((), ())), preferred_element_type=jnp.float32
    )
    router_grad = lax.psum(router_part, ("dp", "expert"))
    part_gateup = acc_gateup.astype(jnp.bfloat16)
    part_down = acc_down.astype(jnp.bfloat16)
    gate_up_grad, down_grad = (
        lax.psum_scatter(part_gateup[None], "dp", scatter_dimension=1, tiled=True).astype(
            jnp.float32
        ),
        lax.psum_scatter(part_down[None], "dp", scatter_dimension=1, tiled=True).astype(
            jnp.float32
        ),
    )
    return (
        token_grad,
        router_grad,
        gate_up_grad.astype(jnp.bfloat16),
        down_grad.astype(jnp.bfloat16),
    )


def solution(mesh):
    return jax.shard_map(
        per_device,
        mesh=mesh,
        in_specs=(
            P(("dp", "expert"), None),
            P(("dp", "expert"), None),
            P(("dp", "expert")),
            P(),
            P(("dp", "expert"), None),
            P("expert", None, None),
            P("expert", None, None),
        ),
        out_specs=(
            P(("dp", "expert"), None),
            P(),
            P("expert", "dp", None),
            P("expert", "dp", None),
        ),
        check_vma=False,
    )
```

profile of v0, /device:TPU:0, one launch (start us, length us, event | category | flops | bytes accessed | tf_op | source)
XLA Modules:
  0.0 440.1 jit_solution(1820209398362379599)
XLA Ops:
  13.3 2.4 scatter_custom_fusion.1
  15.8 2.4 scatter_custom_fusion
  23.2 4.4 all-to-all-start.2
  29.0 13.1 %all-to-all-done.2 = bf16[4,64,2048]{2,1,0:T(8,128)(2,1)S(1)} async-done(((bf16[4,64,2048]{2,1,0:T(8,128)(2,1)}), bf16[4,64,2048]{2,1,0:T(8,128)(2,1)S(1)}, u32[]{:S(2)}, u32[]{:S(2)}) %all-to-all-start.2) | async-done | bytes 1048608 | tf_op jit(solution)/shard_map/all_to_all | solution.py:79
  42.0 3.5 all-to-all-start.1
  45.6 9.7 %fusion.2 = f32[256,3072]{1,0:T(8,128)} fusion(bf16[256,2048]{1,0:T(8,128)(2,1)S(1)} %bitcast.81, bf16[1,2048,3072]{2,1,0:T(8,128)(2,1)} %param.12), kind=kOutput, calls=%fused_computation.9 | convolution fusion | flops 3221225472 | bytes 16777216 | tf_op jit(solution)/shard_map/dot_general | solution.py:9
  55.2 2.3 multiply_convert_fusion.1
  57.6 2.4 all-to-all-done.1
  60.0 4.8 %fusion.24 = f32[256]{0:T(256)S(1)} fusion(bf16[256,1536]{1,0:T(8,128)(2,1)S(1)} %multiply_convert_fusion.1, bf16[1,1536,2048]{2,1,0:T(8,128)(2,1)} %param.13, bf16[256,2048]{1,0:T(8,128)(2,1)S(1)} %bitcast.80), kind=kOutput, calls=%fused_computation.35 | convolution fusion | flops 1613233920 | bytes 8127488 | tf_op jit(solution)/shard_map/dot_general | solution.py:14
  65.4 3.4 all-to-all-start.4
  69.4 3.0 all-to-all-done.4
  72.4 3.5 gather_fusion.4
  82.8 3.2 all-to-all-start
  91.2 4.4 %fusion.4 = bf16[1,1536,2048]{2,1,0:T(8,128)(2,1)} fusion(bf16[256,1536]{1,0:T(8,128)(2,1)S(1)} %multiply_convert_fusion.1, bf16[256,2048]{1,0:T(8,128)(2,1)S(1)} %fusion.22), kind=kOutput, calls=%fused_computation.13 | convolution fusion | flops 1613758464 | bytes 8126464 | tf_op jit(solution)/shard_map/dot_general | solution.py:18
  96.1 6.0 %multiply_convert_fusion.3 = (bf16[256,1536]{1,0:T(8,128)(2,1)S(1)}, bf16[256,1536]{1,0:T(8,128)(2,1)S(1)}) fusion(f32[256,3072]{1,0:T(8,128)} %fusion.2, bf16[256,2048]{1,0:T(8,128)(2,1)S(1)} %bitcast.85, bf16[1,1536,2048]{2,1,0:T(8,128)(2,1)} %param.13), kind=kOutput, calls=%fused_computation.32 | convolution fusion | flops 1615724544 | bytes 12058624 | tf_op jit(solution)/shard_map/dot_general | solution.py:15
  102.1 6.6 %convert_bitcast_fusion = bf16[1,2048,3072]{2,1,0:T(8,128)(2,1)} fusion(bf16[256,2048]{1,0:T(8,128)(2,1)S(1)} %bitcast.82, bf16[256,1536]{1,0:T(8,128)(2,1)S(1)} %get-tuple-element.31, bf16[256,1536]{1,0:T(8,128)(2,1)S(1)} %get-tuple-element.30), kind=kOutput, calls=%fused_computation.11 | convolution fusion | flops 3230662656 | bytes 15204352 | tf_op jit(solution)/shard_map/dot_general | solution.py:25
  108.7 9.0 %fusion.18 = bf16[256,2048]{1,0:T(8,128)(2,1)} fusion(bf16[1,2048,3072]{2,1,0:T(8,128)(2,1)} %param.12, bf16[256,1536]{1,0:T(8,128)(2,1)S(1)} %get-tuple-element.31, bf16[256,1536]{1,0:T(8,128)(2,1)S(1)} %get-tuple-element.30), kind=kOutput, calls=%fused_computation.22 | convolution fusion | flops 3224895488 | bytes 15204352 | tf_op jit(solution)/shard_map/dot_general | solution.py:28
  117.8 3.9 all-to-all-start.3
  121.7 229.6 %all-reduce.2.cloned.1.call-done = f32[2048,128]{0,1:T(8,128)} async-done(((f32[2048,128]{0,1:T(8,128)}), f32[2048,128]{0,1:T(8,128)}) %all-reduce.2.cloned.1.call-update) | async-done | bytes 1048592 | tf_op jit(solution)/shard_map/psum | solution.py:156
  351.2 2.6 copy.55
  353.8 2.5 gather_fusion.3
  356.3 2.2 gather.29
  358.6 5.6 %convert_reduce_fusion = f32[128,2048]{1,0:T(8,128)S(1)} fusion(bf16[128,4,2048]{2,1,0:T(4,128)(2,1)} %gather.29, pred[128,4]{1,0:T(8,128)(4,1)S(1)} %copy-done.6), kind=kLoop, calls=%fused_computation.18 | loop fusion | flops 2883584 | bytes 3146240 | tf_op jit(solution)/shard_map/reduce_sum | solution.py:148
  365.3 67.3 %reduce-scatter.3.cloned.1.call-done = bf16[1,256,3072]{2,1,0:T(8,128)(2,1)} async-done(((bf16[1,2048,3072]{2,1,0:T(8,128)(2,1)}), bf16[1,256,3072]{2,1,0:T(8,128)(2,1)}) %reduce-scatter.3.cloned.1.call-update) | async-done | bytes 1572880 | tf_op jit(solution)/shard_map/reduce_scatter | solution.py:160
  (97 shorter events, 26.4 us)
Async XLA Ops:
  8.0 10.9 %copy-start = (bf16[128,2048]{1,0:T(8,128)(2,1)S(1)}, bf16[128,2048]{1,0:T(8,128)(2,1)}, u32[]{:S(2)}) copy-start(bf16[128,2048]{1,0:T(8,128)(2,1)} %param.7) | copy-start | bytes 1572868
  10.6 0.6 copy-start.5
  18.2 0.7 copy-start.11
  18.9 1.4 copy-start.2
  23.2 4.4 %copy-start.3 = (bf16[2048,128]{1,0:T(8,128)(2,1)S(1)}, bf16[2048,128]{1,0:T(8,128)(2,1)}, u32[]{:S(2)}) copy-start(bf16[2048,128]{1,0:T(8,128)(2,1)} %param.10) | copy-start | bytes 1572868
  23.2 4.9 %copy-start.7 = (s32[128,4]{0,1:T(4,128)S(1)}, s32[128,4]{0,1:T(4,128)}, u32[]{:S(2)}) copy-start(s32[128,4]{0,1:T(4,128)} %param.11) | copy-start | bytes 6148
  23.2 5.1 %copy-start.12 = (f32[128]{0:T(128)S(1)}, f32[128]{0:T(128)}, u32[]{:S(2)}) copy-start(f32[128]{0:T(128)} %param.9) | copy-start | bytes 1540
  23.2 18.8 %all-to-all-start.2 = ((bf16[4,64,2048]{2,1,0:T(8,128)(2,1)}), bf16[4,64,2048]{2,1,0:T(8,128)(2,1)S(1)}, u32[]{:S(2)}, u32[]{:S(2)}) async-start(bf16[4,64,2048]{2,1,0:T(8,128)(2,1)} %get-tuple-element.38), calls=%async_computation.2 | async-start | bytes 2097152 | tf_op jit(solution)/shard_map/all_to_all | solution.py:79
  28.1 44.3 %copy-start.9 = (s32[1024]{0:T(1024)}, s32[1024]{0:T(1024)S(1)}, u32[]{:S(2)}) copy-start(s32[1024]{0:T(1024)S(1)} %pad_clamp_fusion) | copy-start | bytes 12292
  42.0 17.9 %all-to-all-start.1 = ((bf16[4,64,2048]{2,1,0:T(8,128)(2,1)}), bf16[4,64,2048]{2,1,0:T(8,128)(2,1)S(1)}, u32[]{:S(2)}, u32[]{:S(2)}) async-start(bf16[4,64,2048]{2,1,0:T(8,128)(2,1)} %get-tuple-element.39), calls=%async_computation.1 | async-start | bytes 2097152 | tf_op jit(solution)/shard_map/all_to_all | solution.py:86
  65.4 6.9 %all-to-all-start.4 = ((bf16[4,64,2]{1,2,0:T(2,128)(2,1)}), bf16[4,64,2]{1,2,0:T(2,128)(2,1)S(1)}, u32[]{:S(2)}, u32[]{:S(2)}) async-start(bf16[4,64,2]{1,2,0:T(2,128)(2,1)} %copy.51), calls=%async_computation.4 | async-start | bytes 4096 | tf_op jit(solution)/shard_map/all_to_all | solution.py:127
  77.3 0.6 copy-start.8
  82.8 6.9 %all-to-all-start = ((bf16[4,64,2]{1,2,0:T(2,128)(2,1)}), bf16[4,64,2]{1,2,0:T(2,128)(2,1)S(1)}, u32[]{:S(2)}, u32[]{:S(2)}) async-start(bf16[4,64,2]{1,2,0:T(2,128)(2,1)} %copy.49), calls=%async_computation | async-start | bytes 4096 | tf_op jit(solution)/shard_map/all_to_all | solution.py:93
  86.0 265.2 %all-reduce.2.cloned.1.call-start = ((), (), s32[]{:S(2)}) async-start(), calls=%async_computation.7 | async-start | bytes 2097152 | tf_op jit(solution)/shard_map/psum | solution.py:156
  89.2 276.1 %reduce-scatter.5.cloned.1.call-start = ((), (), s32[]{:S(2)}) async-start(), calls=%async_computation.9 | async-start | bytes 7077888 | tf_op jit(solution)/shard_map/reduce_scatter | solution.py:163
  95.7 336.9 %reduce-scatter.3.cloned.1.call-start = ((), (), s32[]{:S(2)}) async-start(), calls=%async_computation.8 | async-start | bytes 14155776 | tf_op jit(solution)/shard_map/reduce_scatter | solution.py:160
  117.8 236.0 %copy-start.10 = (s32[1024]{0:T(1024)S(1)}, s32[1024]{0:T(1024)}, u32[]{:S(2)}) copy-start(s32[1024]{0:T(1024)} %copy-done.9) | copy-start | bytes 12292
  117.8 236.0 %all-to-all-start.3 = ((bf16[4,64,2048]{2,1,0:T(8,128)(2,1)}), bf16[4,64,2048]{2,1,0:T(8,128)(2,1)S(1)}, u32[]{:S(2)}, u32[]{:S(2)}) async-start(bf16[4,64,2048]{2,1,0:T(8,128)(2,1)} %bitcast.9), calls=%async_computation.3 | async-start | bytes 2097152 | tf_op jit(solution)/shard_map/all_to_all | solution.py:120
  356.3 2.3 copy-start.6
  356.3 76.3 %copy-start.1 = (bf16[128,2048]{1,0:T(8,128)(2,1)S(1)}, bf16[128,2048]{1,0:T(8,128)(2,1)}, u32[]{:S(2)}) copy-start(bf16[128,2048]{1,0:T(8,128)(2,1)} %param.7) | copy-start | bytes 1572868
  358.6 5.6 %copy-start.4 = (bf16[2048,128]{1,0:T(8,128)(2,1)S(1)}, bf16[2048,128]{1,0:T(8,128)(2,1)}, u32[]{:S(2)}) copy-start(bf16[2048,128]{1,0:T(8,128)(2,1)} %param.10) | copy-start | bytes 1572868
Sparse Core Ops, SparseCore 0:
  92.6 258.5 all-reduce.1
Sparse Core Ops, SparseCore 1:
  95.8 123.6 reduce-scatter.4
  223.5 209.1 reduce-scatter.2
where the time goes:
time: 441 us; the launch traced here: 440 us
  waiting for transfers between devices  316 us (72%)
  matrix products  43.3 us (10%)
  local copies, waits for them, and re-layouts  26.9 us (6%)
  other arithmetic  19.7 us (4%)
  starting transfers between devices  18.5 us (4%)
  between operations  15.8 us (4%)
    psum x1, waiting for transfers between devices, per_device(): router_grad = lax.psum(router_part, ('dp', 'expert'))  230 us
    reduce_scatter x1, waiting for transfers between devices, per_device(): lax.psum_scatter(part_gateup[None], 'dp', scatter_dimension=1, tiled=True)  67.3 us
    all_to_all x1, waiting for transfers between devices, per_device(): lax.all_to_all(send_in.reshape(flight, capacity, width), 'expert', split_...  13.1 us
    dot_general x1, matrix products, expert_rows(): pre_act = jnp.dot(rows_in, w_gateup, preferred_element_type=jnp.float32)  9.69 us
    dot_general x1, matrix products, expert_rows(): lax.dot_general(pre_grad, w_gateup, (((1,), (1,)), ((), ())), preferred_e...  9.05 us
  transfers between devices with their start and end apart: 8, of which 6 were waited for; matrix products, arithmetic and copies ran while one was open for 13% of the time, Pallas kernels for 0%

commit v1 on v0

--- a/solution.py
+++ b/solution.py
@@ -153,7 +153,7 @@
     router_part = lax.dot_general(
         tokens, logit_grad, (((0,), (0,)), ((), ())), preferred_element_type=jnp.float32
     )
-    router_grad = lax.psum(router_part, ("dp", "expert"))
+    router_grad = jnp.sum(lax.all_gather(router_part, ("dp", "expert")), axis=0)
     part_gateup = acc_gateup.astype(jnp.bfloat16)
     part_down = acc_down.astype(jnp.bfloat16)
     gate_up_grad, down_grad = (

time: 441 us -> 550 us (1.25)
  waiting for transfers between devices: 316 us -> 383 us
  local copies, waits for them, and re-layouts: 26.9 us -> 55.7 us
  blocking collectives: 0 us -> 23 us
  starting transfers between devices: 18.5 us -> 11.3 us
    psum x1 -> x0, waiting for transfers between devices: 230 us -> none  [per_device(): router_grad = lax.psum(router_part, ('dp', 'expert'))]
    all_gather x0 -> x1, waiting for transfers between devices: none -> 166 us  [per_device(): router_grad = jnp.sum(lax.all_gather(router_part, ('dp', 'expert')), axis=0)]
    reduce_scatter x1, waiting for transfers between devices: 67.3 us -> 195 us  [per_device(): lax.psum_scatter(part_gateup[None], 'dp', scatter_dimension=1, tiled=True)]
    unnamed x28 -> x31, local copies, waits for them, and re-layouts: 4.61 us -> 32.6 us
    all_to_all x0 -> x2, blocking collectives: none -> 23 us  [the longest x1 16.9 us: per_device(): lax.all_to_all(back_rows.reshape(sources, capacity, width), 'expert', spl...]
    all_to_all x2 -> x0, starting transfers between devices: 7.09 us -> none  [the longest x1 3.87 us: per_device(): lax.all_to_all(back_rows.reshape(sources, capacity, width), 'expert', spl...]
    reduce_sum x0 -> x1, other arithmetic: none -> 6.8 us  [per_device(): router_grad = jnp.sum(lax.all_gather(router_part, ('dp', 'expert')), axis=0)]
  transfers between devices with their start and end apart: 8 -> 6, of which waited for: 6 -> 5; matrix products, arithmetic and copies ran while one was open for 13% -> 16% of each run, Pallas kernels for 0% -> 0%
where the time goes in v1:
time: 550 us; the launch traced here: 549 us
  waiting for transfers between devices  383 us (70%)
  local copies, waits for them, and re-layouts  55.7 us (10%)
  matrix products  39.1 us (7%)
  blocking collectives  23 us (4%)
  other arithmetic  20.6 us (4%)
  between operations  15.8 us (3%)
  starting transfers between devices  11.3 us (2%)
    reduce_scatter x1, waiting for transfers between devices, per_device(): lax.psum_scatter(part_gateup[None], 'dp', scatter_dimension=1, tiled=True)  195 us
    all_gather x1, waiting for transfers between devices, per_device(): router_grad = jnp.sum(lax.all_gather(router_part, ('dp', 'expert')), axis=0)  166 us
    unnamed x31, local copies, waits for them, and re-layouts  32.6 us
    all_to_all x1, blocking collectives, per_device(): lax.all_to_all(back_rows.reshape(sources, capacity, width), 'expert', spl...  16.9 us
    all_to_all x1, waiting for transfers between devices, per_device(): lax.all_to_all(send_in.reshape(flight, capacity, width), 'expert', split_...  13.1 us
  transfers between devices with their start and end apart: 6, of which 5 were waited for; matrix products, arithmetic and copies ran while one was open for 16% of the time, Pallas kernels for 0%

profile of v1, /device:TPU:0, one launch (start us, length us, event | category | flops | bytes accessed | tf_op | source)
XLA Modules:
  0.0 548.9 jit_solution(1274616684275924743)
XLA Ops:
  13.3 2.4 scatter_custom_fusion.1
  15.8 2.4 scatter_custom_fusion
  23.2 4.4 all-to-all-start.2
  28.9 13.1 %all-to-all-done.2 = bf16[4,64,2048]{2,1,0:T(8,128)(2,1)S(1)} async-done(((bf16[4,64,2048]{2,1,0:T(8,128)(2,1)}), bf16[4,64,2048]{2,1,0:T(8,128)(2,1)S(1)}, u32[]{:S(2)}, u32[]{:S(2)}) %all-to-all-start.2) | async-done | bytes 1048608 | tf_op jit(solution)/shard_map/all_to_all | solution.py:79
  42.0 3.5 all-to-all-start.1
  45.6 6.4 %fusion.2 = f32[256,3072]{1,0:T(8,128)S(1)} fusion(bf16[256,2048]{1,0:T(8,128)(2,1)S(1)} %bitcast.87, bf16[1,2048,3072]{2,1,0:T(8,128)(2,1)} %param.12), kind=kOutput, calls=%fused_computation.10 | convolution fusion | flops 3221225472 | bytes 16777216 | tf_op jit(solution)/shard_map/dot_general | solution.py:9
  54.1 5.9 %all-to-all-done.1 = bf16[4,64,2048]{2,1,0:T(8,128)(2,1)S(1)} async-done(((bf16[4,64,2048]{2,1,0:T(8,128)(2,1)}), bf16[4,64,2048]{2,1,0:T(8,128)(2,1)S(1)}, u32[]{:S(2)}, u32[]{:S(2)}) %all-to-all-start.1) | async-done | bytes 1048608 | tf_op jit(solution)/shard_map/all_to_all | solution.py:86
  59.9 4.7 fusion.24
  65.3 3.2 all-to-all-start.4
  69.1 3.1 all-to-all-done.4
  72.3 3.5 gather_fusion.4
  82.4 6.1 %all_to_all.25 = bf16[4,64,2]{1,2,0:T(2,128)(2,1)S(1)} all-to-all(bf16[4,64,2]{1,2,0:T(2,128)(2,1)S(1)} %copy.47), channel_id=1, replica_groups=mesh['dp'=8,'expert'=4] {'expert'}, dimensions={0} | all-to-all | bytes 2048 | tf_op jit(solution)/shard_map/all_to_all | solution.py:93
  90.0 4.5 fusion.4
  94.9 6.0 %multiply_convert_fusion.3 = (bf16[256,1536]{1,0:T(8,128)(2,1)S(1)}, bf16[256,1536]{1,0:T(8,128)(2,1)S(1)}) fusion(f32[256,3072]{1,0:T(8,128)} %copy-done.3, bf16[256,2048]{1,0:T(8,128)(2,1)S(1)} %bitcast.91, bf16[1,1536,2048]{2,1,0:T(8,128)(2,1)} %param.13), kind=kOutput, calls=%fused_computation.33 | convolution fusion | flops 1615724544 | bytes 12058624 | tf_op jit(solution)/shard_map/dot_general | solution.py:15
  100.9 6.7 %convert_bitcast_fusion = bf16[1,2048,3072]{2,1,0:T(8,128)(2,1)} fusion(bf16[256,2048]{1,0:T(8,128)(2,1)S(1)} %bitcast.88, bf16[256,1536]{1,0:T(8,128)(2,1)S(1)} %get-tuple-element.23, bf16[256,1536]{1,0:T(8,128)(2,1)S(1)} %get-tuple-element.22), kind=kOutput, calls=%fused_computation.12 | convolution fusion | flops 3230662656 | bytes 15204352 | tf_op jit(solution)/shard_map/dot_general | solution.py:25
  107.7 8.1 %fusion.18 = bf16[256,2048]{1,0:T(8,128)(2,1)S(1)} fusion(bf16[1,2048,3072]{2,1,0:T(8,128)(2,1)} %param.12, bf16[256,1536]{1,0:T(8,128)(2,1)S(1)} %get-tuple-element.23, bf16[256,1536]{1,0:T(8,128)(2,1)S(1)} %get-tuple-element.22), kind=kOutput, calls=%fused_computation.23 | convolution fusion | flops 3224895488 | bytes 15204352 | tf_op jit(solution)/shard_map/dot_general | solution.py:28
  115.8 16.9 %all_to_all.26 = bf16[4,64,2048]{2,1,0:T(8,128)(2,1)S(1)} all-to-all(bf16[4,64,2048]{2,1,0:T(8,128)(2,1)S(1)} %bitcast.92), channel_id=1, replica_groups=mesh['dp'=8,'expert'=4] {'expert'}, dimensions={0} | all-to-all | bytes 2097152 | tf_op jit(solution)/shard_map/all_to_all | solution.py:120
  132.6 3.3 gather_fusion.3
  136.0 2.7 gather.29
  138.7 3.9 convert_reduce_fusion
  143.8 166.0 %all-gather.3.cloned.1.call-done = f32[65536,128]{0,1:T(8,128)} async-done(((f32[2048,128]{0,1:T(8,128)}), f32[65536,128]{0,1:T(8,128)}) %all-gather.3.cloned.1.call-update) | async-done | bytes 33554448 | tf_op jit(solution)/shard_map/all_gather | solution.py:156
  309.8 28.2 %copy.55 = f32[16,8,32,2048]{3,2,1,0:T(8,128)S(1)} copy(f32[16,8,32,2048]{3,1,2,0:T(8,128)} %bitcast.85) | data formatting | bytes 67108864
  338.0 6.8 %bitcast_reduce_fusion = f32[2048,128]{0,1:T(8,128)S(1)} fusion(f32[16,8,32,2048]{3,2,1,0:T(8,128)S(1)} %copy.55), kind=kLoop, calls=%fused_computation.7 | loop fusion | flops 8126464 | bytes 34603008 | tf_op jit(solution)/shard_map/reduce_sum | solution.py:156
  346.2 195.3 %reduce-scatter.3.cloned.1.call-done = bf16[1,256,3072]{2,1,0:T(8,128)(2,1)} async-done(((bf16[1,2048,3072]{2,1,0:T(8,128)(2,1)}), bf16[1,256,3072]{2,1,0:T(8,128)(2,1)}) %reduce-scatter.3.cloned.1.call-update) | async-done | bytes 1572880 | tf_op jit(solution)/shard_map/reduce_scatter | solution.py:160
  (99 shorter events, 25.8 us)
Async XLA Ops:
  8.0 10.9 %copy-start = (bf16[128,2048]{1,0:T(8,128)(2,1)S(1)}, bf16[128,2048]{1,0:T(8,128)(2,1)}, u32[]{:S(2)}) copy-start(bf16[128,2048]{1,0:T(8,128)(2,1)} %param.7) | copy-start | bytes 1572868
  10.6 0.6 copy-start.6
  18.2 0.7 copy-start.11
  18.9 1.4 copy-start.2
  23.2 4.4 copy-start.4
  23.2 4.9 copy-start.8
  23.2 5.1 copy-start.13
  23.2 18.8 %all-to-all-start.2 = ((bf16[4,64,2048]{2,1,0:T(8,128)(2,1)}), bf16[4,64,2048]{2,1,0:T(8,128)(2,1)S(1)}, u32[]{:S(2)}, u32[]{:S(2)}) async-start(bf16[4,64,2048]{2,1,0:T(8,128)(2,1)} %get-tuple-element.30), calls=%async_computation.2 | async-start | bytes 2097152 | tf_op jit(solution)/shard_map/all_to_all | solution.py:79
  28.1 44.2 %copy-start.9 = (s32[1024]{0:T(1024)}, s32[1024]{0:T(1024)S(1)}, u32[]{:S(2)}) copy-start(s32[1024]{0:T(1024)S(1)} %pad_clamp_fusion) | copy-start | bytes 12292
  42.0 17.9 %all-to-all-start.1 = ((bf16[4,64,2048]{2,1,0:T(8,128)(2,1)}), bf16[4,64,2048]{2,1,0:T(8,128)(2,1)S(1)}, u32[]{:S(2)}, u32[]{:S(2)}) async-start(bf16[4,64,2048]{2,1,0:T(8,128)(2,1)} %get-tuple-element.31), calls=%async_computation.1 | async-start | bytes 2097152 | tf_op jit(solution)/shard_map/all_to_all | solution.py:86
  52.0 1.6 copy-start.3
  65.3 6.9 %all-to-all-start.4 = ((bf16[4,64,2]{1,2,0:T(2,128)(2,1)}), bf16[4,64,2]{1,2,0:T(2,128)(2,1)S(1)}, u32[]{:S(2)}, u32[]{:S(2)}) async-start(bf16[4,64,2]{1,2,0:T(2,128)(2,1)} %copy.49), calls=%async_computation.4 | async-start | bytes 4096 | tf_op jit(solution)/shard_map/all_to_all | solution.py:127
  68.5 241.3 %all-gather.3.cloned.1.call-start = ((), (), s32[]{:S(2)}) async-start(), calls=%async_computation.9 | async-start | bytes 34603008 | tf_op jit(solution)/shard_map/all_gather | solution.py:156
  76.9 5.3 copy-start.12
  79.8 266.4 %reduce-scatter.5.cloned.1.call-start = ((), (), s32[]{:S(2)}) async-start(), calls=%async_computation.8 | async-start | bytes 7077888 | tf_op jit(solution)/shard_map/reduce_scatter | solution.py:163
  94.5 447.0 %reduce-scatter.3.cloned.1.call-start = ((), (), s32[]{:S(2)}) async-start(), calls=%async_computation.7 | async-start | bytes 14155776 | tf_op jit(solution)/shard_map/reduce_scatter | solution.py:160
  115.8 16.9 %copy-start.10 = (s32[1024]{0:T(1024)S(1)}, s32[1024]{0:T(1024)}, u32[]{:S(2)}) copy-start(s32[1024]{0:T(1024)} %copy-done.9) | copy-start | bytes 12292
  135.9 2.8 copy-start.7
  138.7 3.9 copy-start.5
  338.0 203.4 %copy-start.1 = (bf16[128,2048]{1,0:T(8,128)(2,1)S(1)}, bf16[128,2048]{1,0:T(8,128)(2,1)}, u32[]{:S(2)}) copy-start(bf16[128,2048]{1,0:T(8,128)(2,1)} %param.7) | copy-start | bytes 1572868
Sparse Core Ops, SparseCore 0:
  79.9 229.8 all-gather.2
Sparse Core Ops, SparseCore 1:
  94.6 236.5 reduce-scatter.4
  335.2 206.2 reduce-scatter.2
